TPU v7x, 32 devices: a whole 2x2x4 slice. The times are simulated.
32 devices in a mesh: expert: 4 (over z), context: 8 (over y, x, core).
Axes of the slice: x: 2, y: 2, z: 4, core: 2. Of those that a mesh axis runs over, the one named last changes fastest.
Arguments:
- hidden_in: bfloat16 [4, 3072, 768], P('expert', 'context'), may hold values from -6 to 6
- prior_logits: float32 [4, 3072, 12], P('expert', 'context'), may hold values from -6 to 6
- routes: int32 [4, 3072, 2], P('expert', 'context'), may hold values from 0 to 11, all different within a row; in each aligned block of 384 rows (0 to 383, 384 to 767, ..., all dimensions but the last counted through in order) at most 96 rows name the same one
- block_ids: int32 [4, 3072], P('expert', 'context'), may hold values from 0 to 23, never falling along the last dimension, each value on 1 to 256 neighbouring positions
- grad_out: bfloat16 [4, 3072, 768], P('expert', 'context'), may hold values from -6 to 6
- attn_gain: float32 [768], replicated, may hold values from 0.25 to 1.75
- query_weight: bfloat16 [768, 768], P('context'), may hold values from -0.21875 to 0.21875
- key_weight: bfloat16 [768, 768], P('context'), may hold values from -0.21875 to 0.21875
- value_weight: bfloat16 [768, 768], P('context'), may hold values from -0.21875 to 0.21875
- output_weight: bfloat16 [768, 768], P('context'), may hold values from -0.875 to 0.875
- moe_gain: float32 [768], replicated, may hold values from 0.25 to 1.75
- router_weight: float32 [768, 12], replicated, may hold values from -0.109375 to 0.109375
- prior_weight: float32 [12, 12], replicated, may hold values from -0.875 to 0.875
- const_mix: float32 [2, 2, 768], replicated, may hold values from -0.21875 to 0.21875
- const_vector: float32 [2, 768], replicated, may hold values from -6 to 6
- gate_weight: bfloat16 [8, 768, 2048], P('expert', 'context'), may hold values from -0.21875 to 0.21875
- up_weight: bfloat16 [8, 768, 2048], P('expert', 'context'), may hold values from -0.21875 to 0.21875
- down_weight: bfloat16 [8, 2048, 768], P('expert', 'context'), may hold values from -1 to 1
Outputs:
- layer_out: bfloat16 [4, 3072, 768], P('expert', 'context')
- grad_input: float32 [4, 3072, 768], P('expert', 'context')
- grad_prior: float32 [4, 3072, 12], P('expert', 'context')
- grad_attn_gain: float32 [768], P('context')
- grad_query: float32 [768, 768], P('context')
- grad_key: float32 [768, 768], P('context')
- grad_value: float32 [768, 768], P('context')
- grad_output_weight: float32 [768, 768], P('context')
- grad_moe_gain: float32 [768], P('context')
- grad_router: float32 [768, 12], P('context')
- grad_prior_weight: float32 [12, 12], replicated
- grad_const_mix: float32 [2, 2, 768], P(None, None, 'context')
- grad_const_vector: float32 [2, 768], P(None, 'context')
- grad_gate: float32 [8, 768, 2048], P('expert', 'context')
- grad_up: float32 [8, 768, 2048], P('expert', 'context')
- grad_down: float32 [8, 2048, 768], P('expert', 'context')
Inputs may be any that keep to these rules, and one draw needn't show every extreme that they name: `routes`: each token names two different experts; experts 0 to 7 are feed-forward, 8 the zero expert, 9 the copy expert, the rest constant experts. Among the 384 positions of one device (aligned blocks of 384 positions of a sequence), no expert is named by more than 96 tokens, and in some block one is named by exactly 96. `block_ids`: along a sequence the block id never falls; each id covers 1 to 256 consecutive positions, and some id covers exactly 256.
All inputs are finite; a program needn't handle non-finite values.
Results may differ from a plain program's by a relative error of at most 0.017.
Values may be sent and summed in bfloat16 or wider, within the bound.
A program may use at most 384 MiB of HBM per device.

v0:
```python
import functools
import math

import jax
import jax.numpy as jnp
from jax import lax
from jax.experimental import pallas as pl
from jax.experimental.pallas import tpu as pltpu
from jax.sharding import PartitionSpec as P

HEADS = 12
FFN_E = 8
CAP = 96
TILE = 256
EXTRA = 16
HIDDEN_TILE = 256

EPS = 1e-06
THETA = 10000.0
NEGATIVE = -1e30
HIGH = lax.Precision.HIGHEST
F32 = jnp.float32
BF16 = jnp.bfloat16


def dot(left, right, left_dim=1, right_dim=0):
    return lax.dot_general(
        left, right, (((left_dim,), (right_dim,)), ((), ())), preferred_element_type=F32
    )


def turn(rows, cos_rows, sin_rows, heads, size, back=False):
    half = size // 2
    parts = []
    for head in range(heads):
        first = rows[head * size : head * size + half]
        second = rows[head * size + half : (head + 1) * size]
        if back:
            parts.append(first * cos_rows + second * sin_rows)
            parts.append(second * cos_rows - first * sin_rows)
        else:
            parts.append(first * cos_rows - second * sin_rows)
            parts.append(second * cos_rows + first * sin_rows)
    return jnp.concatenate(parts, axis=0)


def own_tile(index, ranks):
    rank = lax.rem(lax.axis_index("context"), ranks)
    place = lax.rem(index, 2)
    return (index // 2) * (2 * ranks) + jnp.where(place == 0, rank, 2 * ranks - 1 - rank)


def granule_of(slot, ranks):
    return own_tile(slot // 2, ranks) * 2 + lax.rem(slot, 2)


def owner_rank(granule, ranks):
    spot = lax.rem(granule // 2, 2 * ranks)
    return jnp.minimum(spot, 2 * ranks - 1 - spot)


def owner_slot(granule, ranks):
    tile = granule // 2
    upper = jnp.where(lax.rem(tile, 2 * ranks) >= ranks, 1, 0)
    return (tile // (2 * ranks) * 2 + upper) * 2 + lax.rem(granule, 2)


def here_or_away(device, source, target, send, recv):
    place = lax.axis_index("context")

    @pl.when(device == place)
    def _():
        pltpu.make_async_copy(source, target, recv).start()

    @pl.when(device != place)
    def _():
        remote(source, target, send, recv, {"context": device}).start()


def wait_sent(device, source, target, send, recv):
    @pl.when(device != lax.axis_index("context"))
    def _():
        remote(source, target, send, recv, {"context": device}).wait_send()


def wait_landed(device, source, target, send, recv):
    place = lax.axis_index("context")

    @pl.when(device == place)
    def _():
        pltpu.make_async_copy(source, target, recv).wait()

    @pl.when(device != place)
    def _():
        remote(source, target, send, recv, {"context": device}).wait_recv()


def lanes(start):
    return span(start, TILE)


def span(start, size):
    return pl.ds(pl.multiple_of(start * size, size), size)


def cost(micros):
    return pl.CostEstimate(flops=micros * 1_150_000_000, bytes_accessed=0, transcendentals=0)


def vmem(count):
    return [pl.BlockSpec(memory_space=pltpu.VMEM)] * count


def hbm(count):
    return [pl.BlockSpec(memory_space=pl.ANY)] * count


def params(number=None, limit=60):
    if number is None:
        return pltpu.CompilerParams(vmem_limit_bytes=limit << 20)
    return pltpu.CompilerParams(
        collective_id=number, has_side_effects=True, vmem_limit_bytes=limit << 20
    )


def remote(source, target, send, recv, device):
    return pltpu.make_async_remote_copy(
        src_ref=source, dst_ref=target, send_sem=send, recv_sem=recv,
        device_id=device, device_id_type=pl.DeviceIdType.MESH,
    )


def chip_at(chip, far, chips, square, back=False):
    if square:
        x, y = lax.rem(chip, 2), chip // 2
        x = x + (far % 2) * (1 - 2 * x)
        y = y + (far // 2) * (1 - 2 * y)
        return 2 * y + x
    return lax.rem(chip + (chips - far if back else far), chips)


def meet(context, owners):
    place, row = lax.axis_index("context"), lax.axis_index("expert")
    barrier = pltpu.get_barrier_semaphore()
    for far in range(1, context):
        pl.semaphore_signal(
            barrier, inc=1, device_id={"context": lax.rem(place + far, context)},
            device_id_type=pl.DeviceIdType.MESH,
        )
    for far in range(1, owners):
        pl.semaphore_signal(
            barrier, inc=1, device_id={"expert": lax.rem(row + far, owners)},
            device_id_type=pl.DeviceIdType.MESH,
        )
    pl.semaphore_wait(barrier, context + owners - 2)
    return place, row


def attn_forward_kernel(
    dims,
    hidden_ref, gain_ref, own_ids_ref, routes_ref, cotangent_ref, cos_base_ref, sin_base_ref,
    query_w_ref, key_w_ref, value_w_ref, output_ref, gate_ref, up_ref,
    out_t_ref, lse_ref, query_t_ref, ids_all_ref, wt_ref, cos_ref, sin_ref, slots_ref,
    key_out, key_t_out, value_out, a_out, mix_ref,
    output_all_ref, wide_ref, grads_all_ref, stage_ref,
    w_all_ref, value_t_ref, scores_ref, acc_ref, key_ref, key_t_ref, value_ref, a_ref, out_ref,
    ids_ref, pieces_ref, input_ref, grads_ref, keep_sem, granule_send, granule_recv,
    local_sem, send_sem, recv_sem, pass_sem, land_sem, half_send, half_recv,
    row_send, row_recv, hop_send, hop_recv, lend_send, lend_recv, wide_send, wide_recv,
):
    heads, size, ranks, scale, context, owners, roles, square = dims
    length = a_ref.shape[0]
    rows = length // context
    shard = output_ref.shape[0]
    half = wide_ref.shape[2]
    width = heads * size
    tiles = length // TILE
    own_tiles = tiles // ranks
    ext = size + EXTRA
    chips = context // 2
    chunk = 128

    def normalize(step, carry):
        at = span(step, chunk)
        values = hidden_ref[at, :].astype(F32)
        inverse = lax.rsqrt(jnp.mean(values * values, axis=1, keepdims=True) + EPS)
        input_ref[at, :] = (values * inverse * gain_ref[...]).astype(BF16)
        return carry

    lax.fori_loop(0, rows // chunk, normalize, 0)
    ids_ref[...] = jnp.broadcast_to(own_ids_ref[...].astype(F32), ids_ref.shape)
    for which, weight in enumerate((query_w_ref, key_w_ref, value_w_ref)):
        for group in range(context // ranks):
            columns = weight[:, group * width : (group + 1) * width].astype(F32)
            pieces_ref[group, which * width : (which + 1) * width, :] = columns.T.astype(BF16)
    place, row = meet(context, owners)
    chip, core = place // 2, lax.rem(place, 2)
    partner = place + 1 - 2 * core
    slot = chip // (chips // roles)
    other = (roles - 1) - slot
    twin = 2 * lax.rem(chip + chips // 2, chips) + core

    def source(item, device):
        return (ids_ref, pieces_ref.at[device // ranks], input_ref, output_ref)[item]

    def target(item, device):
        return (
            ids_all_ref.at[:, span(device, rows)],
            w_all_ref.at[device],
            a_ref.at[span(device, rows), :],
            output_all_ref.at[span(device, shard), :],
        )[item]

    def from_chip(far):
        return 2 * chip_at(chip, far, chips, square, True) + core

    def sends(item, far):
        if isinstance(far, int) and far == 0:
            peer = partner
        else:
            peer = 2 * chip_at(chip, far, chips, square) + core
        return remote(
            source(item, peer), target(item, place), send_sem.at[item, far],
            recv_sem.at[item, far], {"context": peer},
        )

    def passes(item, far):
        block = target(item, from_chip(far))
        return remote(
            block, block, pass_sem.at[item, far], land_sem.at[item, far], {"context": partner}
        )

    def keeps(item):
        return pltpu.make_async_copy(
            source(item, place), target(item, place), local_sem.at[item]
        )

    def halves(far):
        upper = rows // 2
        start = from_chip(far) * rows + (far - 1) * upper
        block = a_ref.at[pl.ds(pl.multiple_of(start, upper), upper), :]
        return remote(
            block, block, half_send.at[far], half_recv.at[far],
            {"context": 2 * chip_at(chip, 3 - far, chips, square) + core},
        )

    def corner(far):
        upper = rows // 2
        start = from_chip(3) * rows + (far - 1) * upper
        block = a_ref.at[pl.ds(pl.multiple_of(start, upper), upper), :]
        return remote(block, block, half_send.at[far], half_recv.at[far], {"context": partner})

    direct = {item: list(range(1, chips)) for item in range(4)}
    if square:
        direct[2] = [1, 2]
    def begin(item):
        for far in direct[item] + [0]:
            sends(item, far).start()
        keeps(item).start()

    for item in range(3):
        begin(item)

    experts_iota = lax.broadcasted_iota(jnp.int32, (16, rows), 0)
    first_hot = (experts_iota == routes_ref[0:1, :]).astype(F32)
    second_hot = (experts_iota == routes_ref[1:2, :]).astype(F32)
    earlier = lax.broadcasted_iota(jnp.int32, (rows, rows), 0) < lax.broadcasted_iota(
        jnp.int32, (rows, rows), 1
    )
    before = dot((first_hot + second_hot).astype(BF16), earlier.astype(F32).astype(BF16))
    spots = experts_iota.astype(F32) * CAP + before
    slot_lines = []
    for which, hot in enumerate((first_hot, second_hot)):
        found = jnp.sum(hot * spots, axis=0, keepdims=True)
        slot_lines.append(jnp.where(routes_ref[which : which + 1, :] < FFN_E, found, -1.0))
    slots_ref[...] = jnp.concatenate(slot_lines + [jnp.zeros((6, rows), F32)], axis=0)
    per_owner = grads_ref.shape[1] * grads_ref.shape[2]

    def pick_rows(owner, carry):
        places = lax.broadcasted_iota(jnp.int32, (per_owner, rows), 0) + owner * per_owner
        places = places.astype(F32)
        hit = jnp.logical_or(places == slots_ref[0:1, :], places == slots_ref[1:2, :])
        picked = dot(hit.astype(F32).astype(BF16), cotangent_ref[...])
        grads_ref[owner] = picked.astype(BF16).reshape(grads_ref.shape[1:])
        return carry

    lax.fori_loop(0, owners, pick_rows, 0)
    shard_granules = rows // (TILE // 2)
    group = place // ranks
    owned = out_ref.shape[0]

    def outgoing(step):
        granule = granule_of(step, ranks)
        target_slot = group * shard_granules + lax.rem(granule, shard_granules)
        return (
            granule // shard_granules, out_ref.at[step], mix_ref.at[target_slot],
            granule_send.at[step], granule_recv.at[target_slot],
        )

    def part(device, which):
        return grads_ref.at[device, which]

    to_rows, hops, lends = {}, {}, {}
    for far in range(owners):
        peer = lax.rem(row + far, owners)
        spots = [(slot, grads_all_ref.at[slot, core, row])]
        if roles > 1:
            spots.append((other, stage_ref.at[row]))
        for which, (role, spot) in enumerate(spots):
            if far > 0:
                to_rows[which, far] = remote(
                    part(peer, role), spot, row_send.at[which, far], row_recv.at[which, far],
                    {"expert": peer},
                )
            elif which == 0:
                to_rows[which, far] = pltpu.make_async_copy(part(row, role), spot, local_sem.at[4])
            else:
                lends[0] = remote(
                    part(row, role), grads_all_ref.at[slot, core, row], lend_send.at[0],
                    lend_recv.at[0], {"context": twin},
                )
    wide_out, wide_on = [], []
    for which, weight in enumerate((gate_ref, up_ref)):
        spot = wide_ref.at[which, span(place, shard), :]

        def block(device):
            role = device // 2 // (chips // roles)
            return weight.at[role, :, span(lax.rem(device, 2), half)]

        if square:
            peers = [
                (2 * chip_at(chip, far, chips, square) + side, 2 * far + turned)
                for far in (1, 2)
                for turned, side in enumerate((core, 1 - core))
            ] + [(partner, 1)]
        else:
            peers = [(lax.rem(place + far, context), far) for far in range(1, context)]
        for peer, index in peers:
            wide_out.append(
                remote(
                    block(peer), spot, wide_send.at[which, index], wide_recv.at[which, index],
                    {"context": peer},
                )
            )
        wide_out.append(pltpu.make_async_copy(block(place), spot, local_sem.at[5 + which]))
        if square:
            for turned in range(2):
                side = core if turned == 0 else 1 - core
                giver = 2 * chip_at(chip, 2, chips, square) + side
                block_on = wide_ref.at[which, span(giver, shard), :]
                wide_on.append(
                    remote(
                        block_on, block_on, wide_send.at[which, 6 + turned],
                        wide_recv.at[which, 6 + turned],
                        {"context": 2 * chip_at(chip, 1, chips, square) + core},
                    )
                )
    arrives = {}
    if square:
        index = 0
        for which in range(2):
            for far in (1, 2):
                for turned in range(2):
                    arrives[which, far, turned] = wide_out[index]
                    index += 1
            index += 2

    tail = (lax.broadcasted_iota(jnp.int32, (EXTRA, rows), 0) == 0).astype(BF16)
    for item in range(2):
        for far in range(1, chips):
            sends(item, far).wait_recv()
            passes(item, far).start()
        sends(item, 0).wait_recv()
        keeps(item).wait()
        for far in range(1, chips):
            passes(item, far).wait_recv()
    for copy in to_rows.values():
        copy.start()
    for device in range(context):
        wt_ref[:, device * shard : (device + 1) * shard] = w_all_ref[device]

    def project(step, carry):
        far, second = step // 2, lax.rem(step, 2)
        block = 2 * chip_at(chip, far, chips, square, True) + jnp.where(
            second == 0, core, 1 - core
        )

        @pl.when(jnp.logical_and(far == 0, second == 0))
        def _():
            keeps(2).wait()

        @pl.when(jnp.logical_and(far == 0, second == 1))
        def _():
            sends(2, 0).wait_recv()

        if square:

            @pl.when(jnp.logical_and(far == 1, second == 0))
            def _():
                for near in (1, 2):
                    sends(2, near).wait_recv()
                    halves(near).start()
                    passes(2, near).start()
                begin(3)
                for copy in wide_out:
                    copy.start()

            @pl.when(jnp.logical_and(far == 3, second == 0))
            def _():
                for near in (1, 2):
                    corner(near).wait_recv()
                passes(2, 3).start()

        else:

            @pl.when(jnp.logical_and(far > 0, second == 0))
            def _():
                sends(2, far).wait_recv()
                passes(2, far).start()

        @pl.when(jnp.logical_and(far > 0, second == 1))
        def _():
            passes(2, far).wait_recv()

        at = span(block, rows)
        devices = lax.broadcasted_iota(jnp.int32, (size // 2, context), 1) == block
        cos_step = jnp.sum(
            jnp.where(devices, cos_base_ref[:, rows:], 0.0), axis=1, keepdims=True
        )
        sin_step = jnp.sum(
            jnp.where(devices, sin_base_ref[:, rows:], 0.0), axis=1, keepdims=True
        )
        cos_rows, sin_rows = cos_base_ref[:, :rows], sin_base_ref[:, :rows]
        cos_ref[:, at] = cos_step * cos_rows - sin_step * sin_rows
        sin_ref[:, at] = sin_step * cos_rows + cos_step * sin_rows
        both = dot(wt_ref[width:, :], a_ref[at, :], 1, 1)
        key_t = turn(both[:width], cos_ref[:, at], sin_ref[:, at], heads, size)
        key_t_ref[:, at] = key_t.astype(BF16)
        value_t = both[width:]
        for head in range(heads):
            here = slice(head * size, (head + 1) * size)
            key_ref[head, at, :] = key_t[here].T.astype(BF16)
            value_ref[head, at, :] = value_t[here].T.astype(BF16)
            value_t_ref[head * ext : head * ext + size, at] = value_t[here].astype(BF16)
            value_t_ref[head * ext + size : (head + 1) * ext, at] = tail
        return carry

    lax.fori_loop(0, 2 * chips, project, 0)
    if not square:
        begin(3)
        for copy in wide_out:
            copy.start()
    stored = [
        pltpu.make_async_copy(source, target, keep_sem.at[index])
        for index, (source, target) in enumerate(
            ((key_ref, key_out), (key_t_ref, key_t_out), (value_ref, value_out), (a_ref, a_out))
        )
    ]
    for copy in stored:
        copy.start()
    if roles > 1:
        lends[0].start()
    for far in range(owners):
        peer = lax.rem(row + owners - far, owners)
        home = grads_all_ref.at[slot, core, peer]
        if far > 0:
            to_rows[0, far].wait_recv()
        else:
            to_rows[0, far].wait()
        hops[far] = remote(
            home, home, hop_send.at[0, far], hop_recv.at[0, far], {"context": partner}
        )
        hops[far].start()
        if roles > 1 and far > 0:
            to_rows[1, far].wait_recv()
            lends[far] = remote(
                stage_ref.at[peer], home, lend_send.at[far], lend_recv.at[far],
                {"context": twin},
            )
            lends[far].start()

    def relays():
        for far in range(1, chips):
            sends(3, far).wait_recv()
            passes(3, far).start()
        for far in lends:
            lends[far].wait_recv()
            afar(far).start()

    def afar(far):
        away = grads_all_ref.at[other, core, lax.rem(row + owners - far, owners)]
        return remote(
            away, away, hop_send.at[1, far], hop_recv.at[1, far], {"context": partner}
        )

    def attend(index, carry):
        @pl.when(index > 0)
        def _():
            for step in range(2):
                here_or_away(*outgoing(2 * index - 2 + step))

        @pl.when(index == own_tiles - 1)
        def _():
            relays()

        if square:

            @pl.when(index == own_tiles // 2)
            def _():
                for which in range(2):
                    for turned in range(2):
                        arrives[which, 2, turned].wait_recv()
                for copy in wide_on:
                    copy.start()

        tile = own_tile(index, ranks)
        at = lanes(tile)
        query_t = dot(wt_ref[:width, :], a_ref[at, :], 1, 1)
        query_t = turn(query_t, cos_ref[:, at], sin_ref[:, at], heads, size)
        query_t = query_t.astype(BF16) * jnp.asarray(scale, BF16)
        query_t_ref[:, lanes(index)] = query_t
        query_ids = ids_all_ref[0:1, at]

        def score(step, tops, masked):
            here = lanes(step)
            fresh = []
            if masked:
                allowed = ids_all_ref[:, here].T[:, 0:1] <= query_ids
            for head in range(heads):
                part = dot(key_ref[head, here, :], query_t[head * size : (head + 1) * size])
                if masked:
                    part = jnp.where(allowed, part, NEGATIVE)
                scores_ref[head, here, :] = part
                fresh.append(
                    jnp.maximum(tops[head], jnp.max(part.reshape(TILE // 8, 8, TILE), axis=0))
                )
            return tuple(fresh)

        tops = tuple(jnp.full((8, TILE), NEGATIVE, F32) for _ in range(heads))
        stop = jnp.minimum(tile + 2, tiles)
        tops = lax.fori_loop(0, tile, lambda s, c: score(s, c, False), tops)
        tops = lax.fori_loop(tile, stop, lambda s, c: score(s, c, True), tops)
        peaks = [jnp.max(top, axis=0, keepdims=True) for top in tops]
        acc_ref[...] = jnp.zeros_like(acc_ref)

        def combine(step, carry):
            here = lanes(step)
            for head in range(heads):
                weights = jnp.exp(scores_ref[head, here, :] - peaks[head]).astype(BF16)
                acc_ref[head] += dot(value_t_ref[head * ext : (head + 1) * ext, here], weights)
            return carry

        lax.fori_loop(0, stop, combine, 0)
        parts = []
        for head in range(heads):
            total = acc_ref[head, size : size + 1, :]
            part = acc_ref[head, :size, :] * (1.0 / total)
            lse_ref[head : head + 1, lanes(index)] = peaks[head] + jnp.log(total)
            parts.append(part)
        joined = jnp.concatenate(parts, axis=0)
        out_t_ref[:, lanes(index)] = joined
        turned_out = joined.T.astype(BF16)
        out_ref[2 * index] = turned_out[: TILE // 2]
        out_ref[2 * index + 1] = turned_out[TILE // 2 :]
        return carry

    lax.fori_loop(0, own_tiles, attend, 0)
    for step in range(2):
        here_or_away(*outgoing(2 * own_tiles - 2 + step))
    sends(3, 0).wait_recv()
    keeps(3).wait()
    for far in range(1, chips):
        passes(3, far).wait_recv()
    for item in range(4):
        for far in direct[item] + [0]:
            sends(item, far).wait_send()
        for far in range(1, chips):
            passes(item, far).wait_send()
    if square:
        for far in (1, 2):
            halves(far).wait_send()
    forwarded = [arrives[which, 2, turned] for which, _, turned in arrives if _ == 2]
    for copy in wide_out:
        if any(copy is one for one in forwarded):
            copy.wait_send()
        else:
            copy.wait()
    for (which, far), copy in to_rows.items():
        if far > 0:
            copy.wait_send()
    for copy in lends.values():
        copy.wait_send()
    for copy in wide_on + list(hops.values()) + [afar(far) for far in lends] + stored:
        copy.wait()

    def settle(step, carry):
        wait_sent(*outgoing(step))
        giver_group, spot = step // shard_granules, lax.rem(step, shard_granules)
        giver = giver_group * ranks + owner_rank(place * shard_granules + spot, ranks)
        wait_landed(
            giver, out_ref.at[0], mix_ref.at[step], granule_send.at[0], granule_recv.at[step]
        )
        return carry

    lax.fori_loop(0, owned, settle, 0)


def attn_forward(
    hidden, gain, ids, routes, cotangent, cos_base, sin_base,
    query_weight, key_weight, value_weight, output_weight, gate_weight, up_weight,
    heads, size, ranks, context, owners, roles, number,
):
    rows, model = hidden.shape
    length = rows * context
    own = length // ranks
    width = heads * size
    ext = size + EXTRA
    shard = output_weight.shape[0]
    chips = context // 2
    granule = TILE // 2
    head_shape = jax.ShapeDtypeStruct((heads, length, size), BF16)
    turned_shape = jax.ShapeDtypeStruct((width, length), BF16)
    a_shape = jax.ShapeDtypeStruct((length, model), BF16)
    own_shape = jax.ShapeDtypeStruct((own // granule, granule, width), BF16)
    shapes = (
        jax.ShapeDtypeStruct((width, own), F32),
        jax.ShapeDtypeStruct((heads, own), F32),
        jax.ShapeDtypeStruct((width, own), BF16),
        jax.ShapeDtypeStruct((8, length), F32),
        jax.ShapeDtypeStruct((3 * width, model), BF16),
        jax.ShapeDtypeStruct((size // 2, length), F32),
        jax.ShapeDtypeStruct((size // 2, length), F32),
        jax.ShapeDtypeStruct((8, rows), F32),
        head_shape,
        turned_shape,
        head_shape,
        a_shape,
        own_shape,
        jax.ShapeDtypeStruct((model, model), BF16),
        jax.ShapeDtypeStruct((2, model, gate_weight.shape[2] // 2), BF16),
        jax.ShapeDtypeStruct((roles, 2, owners, CAP, model), BF16),
        jax.ShapeDtypeStruct((owners, CAP, model), BF16),
    )
    square = chips == 4 and roles == 2
    dims = (heads, size, ranks, size ** (-0.5), context, owners, roles, square)
    return pl.pallas_call(
        functools.partial(attn_forward_kernel, dims),
        out_shape=shapes,
        in_specs=vmem(10) + hbm(3),
        out_specs=vmem(8) + hbm(9),
        scratch_shapes=[
            pltpu.VMEM((context, 3 * width, shard), BF16),
            pltpu.VMEM((heads * ext, length), BF16),
            pltpu.VMEM((heads, length, TILE), F32),
            pltpu.VMEM((heads, ext, TILE), F32),
        ]
        + [
            pltpu.VMEM(one.shape, one.dtype)
            for one in (head_shape, turned_shape, head_shape, a_shape, own_shape)
        ]
        + [
            pltpu.VMEM((8, rows), F32),
            pltpu.VMEM((context // ranks, 3 * width, shard), BF16),
            pltpu.VMEM((rows, model), BF16),
            pltpu.VMEM((owners, roles, CAP, model), BF16),
        ]
        + [
            pltpu.SemaphoreType.DMA((4,)),
            pltpu.SemaphoreType.DMA((own // granule,)),
            pltpu.SemaphoreType.DMA((own // granule,)),
            pltpu.SemaphoreType.DMA((7,)),
            pltpu.SemaphoreType.DMA((4, chips)),
            pltpu.SemaphoreType.DMA((4, chips)),
            pltpu.SemaphoreType.DMA((4, chips)),
            pltpu.SemaphoreType.DMA((4, chips)),
            pltpu.SemaphoreType.DMA((3,)),
            pltpu.SemaphoreType.DMA((3,)),
        ]
        + [pltpu.SemaphoreType.DMA((2, owners))] * 4
        + [pltpu.SemaphoreType.DMA((owners,))] * 2
        + [pltpu.SemaphoreType.DMA((2, context))] * 2,
        compiler_params=params(number, 62),
        cost_estimate=cost(80),
        name="attn_forward",
    )(
        hidden, gain, ids, routes, cotangent, cos_base, sin_base,
        query_weight, key_weight, value_weight, output_weight, gate_weight, up_weight,
    )


def attn_backward_kernel(
    dims,
    grad_ref, a_ref, wt_ref, cos_ref, sin_ref, ids_all_ref,
    out_t_ref, lse_ref, query_t_ref, key_ref, key_t_ref, value_ref,
    wide_ref, outs_ref, output_ref,
    da_ref, pieces_ref, output_sum_ref, wide_in_ref, outs_in_ref,
    query_ref, own_grad_ref, dq_ref, dk_ref, dv_ref, grad_w_ref,
    landed_ref, output_in_ref, share_ref, shares_ref,
    granule_send, granule_recv, share_send, share_recv,
    wide_send, wide_recv, output_send, output_recv,
    row_send, row_recv, local_sem,
):
    heads, size, ranks, scale, context, owners, roles = dims
    length = a_ref.shape[0]
    shard = pieces_ref.shape[2]
    width = heads * size
    tiles = length // TILE
    own_tiles = tiles // ranks
    chips = context // 2
    place, row = meet(context, owners)
    chip, core = place // 2, lax.rem(place, 2)
    owned = landed_ref.shape[0]
    shard_granules = owned * ranks // context

    def outgoing(step):
        giver = step // shard_granules
        granule = place * shard_granules + lax.rem(step, shard_granules)
        landing = owner_slot(granule, ranks)
        return (
            giver * ranks + owner_rank(granule, ranks), grad_ref.at[step],
            landed_ref.at[landing], granule_send.at[step], granule_recv.at[landing],
        )

    def launch(step, carry):
        here_or_away(*outgoing(step))
        return carry

    lax.fori_loop(0, owned, launch, 0)
    copies, output_copies = [], []
    for item, (grads, target, send, recv) in enumerate(
        (
            (output_ref, output_in_ref, output_send, output_recv),
            (wide_ref, wide_in_ref, wide_send, wide_recv),
        )
    ):
        for far in range(context):
            peer = lax.rem(place + far, context)
            at = span(peer, shard)
            source = grads.at[:, at, :] if item else grads.at[at, :]
            group_copies = copies if item else output_copies
            if far == 0:
                group_copies.append(
                    pltpu.make_async_copy(source, target.at[place], local_sem.at[item])
                )
            else:
                group_copies.append(
                    remote(
                        source, target.at[place], send.at[far], recv.at[far], {"context": peer}
                    )
                )
    for far in range(owners):
        peer = lax.rem(row + far, owners)
        if far == 0:
            copies.append(
                pltpu.make_async_copy(outs_ref.at[row], outs_in_ref.at[row], local_sem.at[2])
            )
        else:
            copies.append(
                remote(
                    outs_ref.at[peer], outs_in_ref.at[row], row_send.at[far], row_recv.at[far],
                    {"expert": peer},
                )
            )
    dk_ref[...] = jnp.zeros_like(dk_ref)
    dv_ref[...] = jnp.zeros_like(dv_ref)
    da_ref[...] = jnp.zeros_like(da_ref)
    grad_w_ref[...] = jnp.zeros_like(grad_w_ref)
    def landed(step, carry):
        giver = granule_of(step, ranks) // shard_granules
        wait_landed(
            giver, grad_ref.at[0], landed_ref.at[step], granule_send.at[0], granule_recv.at[step]
        )
        return carry

    lax.fori_loop(0, owned, landed, 0)
    for copy in output_copies + copies:
        copy.start()

    def share_copy(far):
        return remote(
            share_ref, shares_ref.at[row], share_send.at[far], share_recv.at[far],
            {"expert": lax.rem(row + far, owners)},
        )

    def attend(index, carry):
        tile = own_tile(index, ranks)
        at = lanes(tile)
        query_t = query_t_ref[:, lanes(index)]
        @pl.when(index == own_tiles // 2)
        def _():
            for copy in output_copies:
                copy.wait()
            total = output_in_ref[0].astype(F32)
            for giver in range(1, context):
                total = total + output_in_ref[giver].astype(F32)
            share_ref[...] = total.astype(BF16)

        @pl.when(index == own_tiles // 2 + 1)
        def _():
            for far in range(1, owners):
                share_copy(far).start()

        grad_rows = landed_ref[pl.ds(2 * index, 2)].reshape(TILE, width)
        grad_t = grad_rows.astype(F32).T
        query_rows = query_t.astype(F32).T.astype(BF16)
        query_ids = ids_all_ref[0:1, at]
        deltas, tops, grads_low = [], [], []
        for head in range(heads):
            rows = slice(head * size, (head + 1) * size)
            query_ref[head] = query_rows[:, rows]
            own_grad_ref[head] = grad_rows[:, rows]
            deltas.append(
                jnp.sum(grad_t[rows] * out_t_ref[rows, lanes(index)], axis=0, keepdims=True)
            )
            tops.append(lse_ref[head : head + 1, lanes(index)])
        grad_t_low = grad_t.astype(BF16)
        dq_ref[...] = jnp.zeros_like(dq_ref)

        def chunk(step, carry, masked):
            here = lanes(step)
            if masked:
                allowed = ids_all_ref[:, here].T[:, 0:1] <= query_ids
            for head in range(heads):
                rows = slice(head * size, (head + 1) * size)
                scores = dot(key_ref[head, here, :], query_t[rows]) - tops[head]
                if masked:
                    scores = jnp.where(allowed, scores, NEGATIVE)
                probs = jnp.exp(scores)
                grad_probs = dot(value_ref[head, here, :], grad_t_low[rows])
                grad_scores = (probs * (grad_probs - deltas[head])).astype(BF16)
                dv_ref[head, here, :] += dot(probs.astype(BF16), own_grad_ref[head])
                dk_ref[head, here, :] += dot(grad_scores, query_ref[head])
                dq_ref[rows, :] += dot(key_t_ref[rows, here], grad_scores)
            return carry

        stop = jnp.minimum(tile + 2, tiles)
        lax.fori_loop(0, tile, lambda s, c: chunk(s, c, False), 0)
        lax.fori_loop(tile, stop, lambda s, c: chunk(s, c, True), 0)
        grad_query = turn(
            dq_ref[...] * scale, cos_ref[:, at], sin_ref[:, at], heads, size, back=True
        )
        grad_w_ref[:width, :] += dot(grad_query.astype(BF16), a_ref[at, :])
        da_ref[at, :] = dot(grad_query.T.astype(BF16), wt_ref[:width, :]).astype(BF16)
        return carry

    lax.fori_loop(0, own_tiles, attend, 0)

    def finish(step, carry):
        at = lanes(step)
        key_grad = jnp.concatenate([dk_ref[head, at, :].T for head in range(heads)], axis=0)
        key_grad = turn(key_grad, cos_ref[:, at], sin_ref[:, at], heads, size, back=True)
        value_grad = jnp.concatenate([dv_ref[head, at, :].T for head in range(heads)], axis=0)
        both = jnp.concatenate([key_grad, value_grad], axis=0)
        grad_w_ref[width:, :] += dot(both.astype(BF16), a_ref[at, :])
        total = da_ref[at, :].astype(F32) + dot(both.T.astype(BF16), wt_ref[width:, :])
        da_ref[at, :] = total.astype(BF16)
        return carry

    lax.fori_loop(0, tiles, finish, 0)
    for piece in range(pieces_ref.shape[0]):
        pieces_ref[piece] = grad_w_ref[:, piece * shard : (piece + 1) * shard].astype(BF16)
    for copy in copies:
        copy.wait()
    for far in range(1, owners):
        share_copy(far).wait()
    shares_ref[row] = share_ref[...]
    total = shares_ref[0].astype(F32)
    for giver in range(1, owners):
        total = total + shares_ref[giver].astype(F32)
    output_sum_ref[...] = total

    def settle(step, carry):
        wait_sent(*outgoing(step))
        return carry

    lax.fori_loop(0, owned, settle, 0)


def attn_backward(
    grad_own, a_full, weights_t, cos_t, sin_t, ids, kept,
    grad_wide, outs, grad_output, heads, size, ranks, context, roles, number,
):
    length, model = a_full.shape
    width = heads * size
    owners = outs.shape[0]
    shard = model // context
    shapes = (
        jax.ShapeDtypeStruct(a_full.shape, BF16),
        jax.ShapeDtypeStruct((context, weights_t.shape[0], shard), BF16),
        jax.ShapeDtypeStruct((shard, model), F32),
        jax.ShapeDtypeStruct((context, 2, shard, grad_wide.shape[2]), BF16),
        jax.ShapeDtypeStruct(outs.shape, BF16),
    )
    dims = (heads, size, ranks, size ** (-0.5), context, owners, roles)
    return pl.pallas_call(
        functools.partial(attn_backward_kernel, dims),
        out_shape=shapes,
        in_specs=vmem(12) + hbm(3),
        out_specs=vmem(3) + hbm(2),
        scratch_shapes=[
            pltpu.VMEM((heads, TILE, size), BF16),
            pltpu.VMEM((heads, TILE, size), BF16),
            pltpu.VMEM((width, TILE), F32),
            pltpu.VMEM((heads, length, size), F32),
            pltpu.VMEM((heads, length, size), F32),
            pltpu.VMEM(weights_t.shape, F32),
            pltpu.VMEM(grad_own.shape, BF16),
            pltpu.VMEM((context, shard, model), BF16),
            pltpu.VMEM((shard, model), BF16),
            pltpu.VMEM((owners, shard, model), BF16),
        ]
        + [pltpu.SemaphoreType.DMA((grad_own.shape[0],))] * 2
        + [pltpu.SemaphoreType.DMA((owners,))] * 2
        + [pltpu.SemaphoreType.DMA((context,))] * 4
        + [pltpu.SemaphoreType.DMA((owners,))] * 2
        + [pltpu.SemaphoreType.DMA((3,))],
        compiler_params=params(number, 63),
        cost_estimate=cost(60),
        name="attn_backward",
    )(
        grad_own, a_full, weights_t, cos_t, sin_t, ids, *kept,
        grad_wide, outs, grad_output,
    )


def moe_kernel(
    context, owners, roles, square,
    gates_ref, rows_ref, grads_hbm, wide_hbm, down_hbm,
    dots_back, grad_back, out_back, grad_wide_out, down_in,
    gates_all, rows_all, rows_stage, grads_ref, wide_ref, down_ref,
    rows_t_ref, dye_ref, out_acc, grad_acc, grad_wide_ref, grad_down_ref,
    dots_ref, grad_low, out_low, dots_twin, grad_twin, out_twin,
    dots_sum, grad_sum, out_sum, dots_relay, grad_relay,
    load_sem, local_sem, send_sem, recv_sem, pass_sem, land_sem, twin_sem, come_sem,
    relay_sem, reach_sem, down_send, down_recv, down_on, back_send, back_recv,
    pair_send, pair_recv, home_send, home_recv, lend_send, lend_recv, on_send, on_recv,
    out_send, out_recv, loan_send, loan_recv,
):
    chips = context // 2
    cap, width = rows_all.shape[1:]
    flat = dye_ref.shape
    loads = [
        pltpu.make_async_copy(source, target, load_sem.at[index])
        for index, (source, target) in enumerate(((grads_hbm, grads_ref), (wide_hbm, wide_ref)))
    ]
    for copy in loads:
        copy.start()
    place, row = meet(context, owners)
    chip, core = place // 2, lax.rem(place, 2)
    partner = {"context": place + 1 - 2 * core}
    slot = chip // (chips // roles)
    other = (roles - 1) - slot
    twin = {"context": 2 * lax.rem(chip + chips // 2, chips) + core}

    def block(spot, side, peer):
        return (spot * 2 + side) * owners + peer

    sent, local, passed, lent, relayed = {}, [], [], {}, []
    for far in range(1, owners):
        peer = lax.rem(row + far, owners)
        pairs = [
            (gates_ref.at[peer], gates_all.at[block(slot, core, row)]),
            (rows_ref.at[peer, slot], rows_all.at[block(slot, core, row)]),
        ]
        if roles > 1:
            pairs.append((rows_ref.at[peer, other], rows_stage.at[row]))
        for item, (source, target) in enumerate(pairs):
            sent[item, far] = remote(
                source, target, send_sem.at[item, far], recv_sem.at[item, far], {"expert": peer}
            )
            sent[item, far].start()
    mine = block(slot, core, row)
    for item, (source, target) in enumerate(
        ((gates_ref.at[row], gates_all.at[mine]), (rows_ref.at[row, slot], rows_all.at[mine]))
    ):
        local.append(pltpu.make_async_copy(source, target, local_sem.at[item]))
        local[-1].start()
        passed.append(
            remote(source, target, pass_sem.at[item, 0], land_sem.at[item, 0], partner)
        )
        passed[-1].start()
    if roles > 1:
        for item, (source, everything) in enumerate(
            ((gates_ref.at[row], gates_all), (rows_ref.at[row, other], rows_all))
        ):
            lent[item, 0] = (
                remote(
                    source, everything.at[mine], twin_sem.at[item, 0], come_sem.at[item, 0], twin
                ),
                everything.at[block(other, core, row)],
            )
            lent[item, 0][0].start()

    half = place // chips
    down_rows = down_hbm.shape[1]
    mark = lax.rem(place, chips)
    spot_down = down_ref.at[span(mark, down_rows), :]

    def down_copy(far, here):
        to_chip = chip_at(chip, far, chips, square)
        source = down_hbm.at[to_chip // (chips // roles)]
        if here:
            return pltpu.make_async_copy(source, spot_down, down_recv.at[mark])
        return remote(
            source, spot_down, down_send.at[far], down_recv.at[mark],
            {"context": 2 * to_chip + half},
        )

    @pl.when(half == core)
    def _():
        down_copy(0, True).start()

    @pl.when(half != core)
    def _():
        down_copy(0, False).start()

    fars = [1, 2] if square else list(range(1, chips))
    for far in fars:
        down_copy(far, False).start()

    def arrival(number):
        wait_landed(
            core * chips + number, down_hbm.at[0], down_ref.at[span(number, down_rows), :],
            down_send.at[0], down_recv.at[number],
        )

    def onward(number):
        land = down_ref.at[span(number, down_rows), :]
        return remote(
            land, land, down_on.at[number], down_recv.at[number],
            {"context": 2 * chip_at(chip, 1, chips, square) + core},
        )

    def from_below(number):
        return (core * chips + number) // 2 == chip_at(chip, 2, chips, square)

    for far in range(1, owners):
        peer = lax.rem(row + owners - far, owners)
        for item, everything in enumerate((gates_all, rows_all)):
            sent[item, far].wait_recv()
            landed = everything.at[block(slot, core, peer)]
            passed.append(
                remote(landed, landed, pass_sem.at[item, far], land_sem.at[item, far], partner)
            )
            passed[-1].start()
            if roles > 1:
                if item == 1:
                    sent[2, far].wait_recv()
                lent[item, far] = (
                    remote(
                        landed if item == 0 else rows_stage.at[peer], landed,
                        twin_sem.at[item, far], come_sem.at[item, far], twin,
                    ),
                    everything.at[block(other, core, peer)],
                )
                lent[item, far][0].start()
        if square and far == 1:
            for number in range(chips):

                @pl.when(from_below(number))
                def _():
                    arrival(number)
                    onward(number).start()

    for (item, far), (copy, arriving) in lent.items():
        copy.wait_recv()
        relayed.append(
            remote(
                arriving, arriving, relay_sem.at[item, far], reach_sem.at[item, far], partner
            )
        )
        relayed[-1].start()
    for number in range(chips):
        if square:

            @pl.when(from_below(number))
            def _():
                onward(number).wait_send()

            @pl.when(jnp.logical_not(from_below(number)))
            def _():
                arrival(number)

        else:
            arrival(number)
    for copy in loads + local:
        copy.wait()
    for copy in passed + relayed:
        copy.wait()

    blocks = roles * 2 * owners
    rows_t_ref[...] = rows_all[...].reshape(flat).astype(F32).T.astype(BF16)

    def scale(number, carry):
        columns = gates_all[number].T[:cap]
        column = columns[:, 0:1]
        if roles > 1:
            column = jnp.where(slot == 0, column, columns[:, 1:2])
        dye_ref[span(number, cap), :] = (grads_ref[number].astype(F32) * column).astype(BF16)
        return carry

    lax.fori_loop(0, blocks, scale, 0)
    out_acc[...] = jnp.zeros_like(out_acc)
    grad_acc[...] = jnp.zeros_like(grad_acc)
    back_rows = down_in.shape[1]
    per_step = HIDDEN_TILE // back_rows
    tiles = wide_ref.shape[2] // HIDDEN_TILE

    def leaving(index):
        return (
            core * chips + index, grad_down_ref.at[index], down_in.at[chip],
            back_send.at[index], back_recv.at[chip],
        )

    def hidden_tile(step, carry):
        tile = lax.rem(step + (1 - lax.rem(chip, 2)) * (tiles // 2), tiles)
        at = span(tile, HIDDEN_TILE)
        rows = rows_all[...].reshape(flat)
        dye = dye_ref[...]
        gate, up, down = wide_ref[0, :, at], wide_ref[1, :, at], down_ref[at, :]
        gate_pre = dot(rows, gate)
        up_pre = dot(rows, up)
        sigmoid = jax.nn.sigmoid(gate_pre)
        silu = gate_pre * sigmoid
        hidden = silu * up_pre
        grad_down = dot(hidden.T.astype(BF16), dye).astype(BF16)
        for index in range(per_step):
            grad_down_ref[tile * per_step + index] = grad_down[
                index * back_rows : (index + 1) * back_rows
            ]
        grad_hidden = dot(dye, down, 1, 1).astype(BF16).astype(F32)
        for index in range(per_step):
            here_or_away(*leaving(tile * per_step + index))
        out_acc[...] += dot(hidden.astype(BF16), down).reshape(out_acc.shape)
        grad_gate = (
            grad_hidden * up_pre * sigmoid * (1.0 + gate_pre * (1.0 - sigmoid))
        ).astype(BF16)
        grad_up = (grad_hidden * silu).astype(BF16)
        grad_wide_ref[0, :, at] = dot(rows_t_ref[...], grad_gate).astype(BF16)
        grad_wide_ref[1, :, at] = dot(rows_t_ref[...], grad_up).astype(BF16)
        total = dot(grad_gate, gate, 1, 1) + dot(grad_up, up, 1, 1)
        grad_acc[...] += total.reshape(grad_acc.shape)
        return carry

    lax.fori_loop(0, tiles, hidden_tile, 0)
    store = pltpu.make_async_copy(grad_wide_ref, grad_wide_out, load_sem.at[2])
    store.start()

    order = list(range(1, owners)) + [0]
    turns = (other, slot) if roles > 1 else (slot,)
    pair, gone, loaned, handed, outs, loans = {}, {}, {}, {}, [], []
    items = (
        (dots_ref, dots_twin, dots_sum, dots_relay, dots_back),
        (grad_low, grad_twin, grad_sum, grad_relay, grad_back),
    )

    def share(which, far):
        spot, peer = turns[which], lax.rem(row + far, owners)
        sources = (dots_ref.at[block(spot, 1 - core, peer)], grad_low.at[spot, peer])
        for item, source in enumerate(sources):
            pair[item, which, far] = remote(
                source, items[item][1].at[spot, peer],
                pair_send.at[item, which, far], pair_recv.at[item, which, far], partner,
            )
            pair[item, which, far].start()

    def line(number):
        product = out_acc[number] * grads_ref[number].astype(F32)
        total = product[:, :128]
        for start in range(128, width, 128):
            total = total + product[:, start : start + 128]
        totals = jnp.sum(total.T, axis=0, keepdims=True)
        dots_ref[number, :, :cap] = jnp.broadcast_to(totals, (8, cap))

    def lower(step, carry):
        spot, peer = step // owners, lax.rem(step, owners)
        number = block(spot, 1 - core, peer)
        grad_low[spot, peer] = grad_acc[number].astype(BF16)
        line(number)
        return carry

    def lower_out(step, carry):
        spot, peer = step // owners, lax.rem(step, owners)
        out_low[spot, peer] = out_acc[block(spot, 1 - core, peer)].astype(BF16)
        line(block(spot, core, peer))
        return carry

    lax.fori_loop(0, roles * owners, lower, 0)
    for far in order:
        for which in range(len(turns)):
            share(which, far)
    lax.fori_loop(0, roles * owners, lower_out, 0)
    for which, spot in enumerate(turns):
        outs.append(
            remote(
                out_low.at[spot], out_twin.at[spot], out_send.at[which], out_recv.at[which],
                partner,
            )
        )
        outs[-1].start()

    def leave(which, far):
        peer = lax.rem(row + far, owners)
        spot = turns[which]
        for item, (_, _, total, relay, back) in enumerate(items):
            if roles > 1 and which == 0:
                target = back.at[row, slot] if far == 0 else relay.at[peer]
                loaned[item, far] = remote(
                    total.at[spot, peer], target, lend_send.at[item, far],
                    lend_recv.at[item, far], twin,
                )
                loaned[item, far].start()
            elif far > 0:
                gone[item, far] = remote(
                    total.at[spot, peer], back.at[row, slot], home_send.at[item, far],
                    home_recv.at[item, far], {"expert": peer},
                )
                gone[item, far].start()

    last = None
    for far in order:
        peer = lax.rem(row + far, owners)
        for which, spot in enumerate(turns):
            number = block(spot, core, peer)
            for item in range(2):
                pair[item, which, far].wait_recv()
            dots_sum[spot, peer] = dots_ref[number] + dots_twin[spot, peer]

            def add(part, carry, number=number, spot=spot, peer=peer):
                at = pl.ds(pl.multiple_of(part * (cap // 3), cap // 3), cap // 3)
                grad_sum[spot, peer, at, :] = (
                    grad_acc[number, at, :] + grad_twin[spot, peer, at, :].astype(F32)
                ).astype(BF16)
                return carry

            lax.fori_loop(0, 3, add, 0)
            if last is not None:
                leave(*last)
            last = (which, far)
    dots_back[row, slot] = dots_sum[slot, row]
    grad_back[row, slot] = grad_sum[slot, row]
    leave(*last)
    if roles > 1:
        for far in range(1, owners):
            peer = lax.rem(row + far, owners)
            for item, (_, _, _, relay, back) in enumerate(items):
                loaned[item, far].wait_recv()
                handed[item, far] = remote(
                    relay.at[peer], back.at[row, other], on_send.at[item, far],
                    on_recv.at[item, far], {"expert": peer},
                )
                handed[item, far].start()
    for which, spot in enumerate(turns):
        outs[which].wait_recv()

        def add_out(peer, carry, which=which, spot=spot):
            summed = out_acc[block(spot, core, peer)] + out_twin[spot, peer].astype(F32)
            if roles > 1 and which == 0:
                out_sum[peer] = summed.astype(BF16)
            else:
                out_back[peer, slot] = summed.astype(BF16)
            return carry

        lax.fori_loop(0, owners, add_out, 0)
    if roles > 1:
        loans.append(remote(out_sum, out_back.at[:, slot], loan_send, loan_recv, twin))
        loans[-1].start()
        for item in range(2):
            loaned[item, 0].wait_recv()
    for copy in sent.values():
        copy.wait_send()
    for copy, _ in lent.values():
        copy.wait_send()
    for far in fars:
        down_copy(far, False).wait_send()

    @pl.when(half != core)
    def _():
        down_copy(0, False).wait_send()

    for index in range(chips):
        wait_sent(*leaving(index))
        wait_landed(
            2 * index + place // chips, grad_down_ref.at[0], down_in.at[index],
            back_send.at[index], back_recv.at[index],
        )
    for copy in list(pair.values()) + outs + list(loaned.values()):
        copy.wait_send()
    for copy in list(gone.values()) + list(handed.values()) + loans + [store]:
        copy.wait()


def moe(gates, rows, grads, wide_full, down_weight, context, roles, number):
    owners, _, cap, width = rows.shape
    chips = context // 2
    hidden = wide_full.shape[2]
    blocks = roles * 2 * owners
    slots = blocks * cap
    line = gates.shape[1:]
    square = chips == 4 and roles == 2
    low = (owners, cap, width)
    back = (chips, hidden // chips, width)
    dma = pltpu.SemaphoreType.DMA
    return pl.pallas_call(
        functools.partial(moe_kernel, context, owners, roles, square),
        out_shape=(
            jax.ShapeDtypeStruct((owners, roles) + line, F32),
            jax.ShapeDtypeStruct((owners, roles, cap, width), BF16),
            jax.ShapeDtypeStruct((owners, roles, cap, width), BF16),
            jax.ShapeDtypeStruct(wide_full.shape, BF16),
            jax.ShapeDtypeStruct(back, BF16),
        ),
        in_specs=vmem(2) + hbm(3),
        out_specs=vmem(3) + hbm(2),
        scratch_shapes=[
            pltpu.VMEM((blocks,) + line, F32),
            pltpu.VMEM((blocks, cap, width), BF16),
            pltpu.VMEM(low, BF16),
            pltpu.VMEM((blocks, cap, width), BF16),
            pltpu.VMEM(wide_full.shape, BF16),
            pltpu.VMEM((hidden, width), BF16),
            pltpu.VMEM((width, slots), BF16),
            pltpu.VMEM((slots, width), BF16),
            pltpu.VMEM((blocks, cap, width), F32),
            pltpu.VMEM((blocks, cap, width), F32),
            pltpu.VMEM(wide_full.shape, BF16),
            pltpu.VMEM(back, BF16),
            pltpu.VMEM((blocks,) + line, F32),
            pltpu.VMEM((roles,) + low, BF16),
            pltpu.VMEM((roles,) + low, BF16),
            pltpu.VMEM((roles, owners) + line, F32),
            pltpu.VMEM((roles,) + low, BF16),
            pltpu.VMEM((roles,) + low, BF16),
            pltpu.VMEM((roles, owners) + line, F32),
            pltpu.VMEM((roles,) + low, BF16),
            pltpu.VMEM(low, BF16),
            pltpu.VMEM((owners,) + line, F32),
            pltpu.VMEM(low, BF16),
            dma((3,)),
            dma((2,)),
        ]
        + [dma((3, owners))] * 8
        + [dma((chips,))] * 5
        + [dma((2, roles, owners))] * 2
        + [dma((2, owners))] * 6
        + [dma((roles,))] * 2
        + [dma] * 2,
        compiler_params=params(number, 62),
        cost_estimate=cost(97),
        name="moe",
    )(gates, rows, grads.reshape(blocks, cap, width), wide_full, down_weight)


def finish_kernel(
    chips, owners, groups,
    da_ref, pieces_ref, small_ref, slots_ref, gates_ref, gain_ref, query_w, key_w, value_w,
    base_hbm, returned_hbm, after_hbm, hidden_hbm,
    layer_ref, total_ref, query_ref, key_ref, value_ref, dots_ref, small_all_ref,
    sums_ref, base_ref, returned_ref, after_ref, hidden_ref, columns_ref, load_sem,
    da_twin, da_sum, da_in, w_twin, w_sum, w_in, s_twin, s_sum, s_in, s_total,
    stack_ref, shares, shares_in, block_ref,
    pair_send, pair_recv, chip_send, chip_recv, row_send, row_recv,
):
    loads = [
        pltpu.make_async_copy(source, target, load_sem.at[index])
        for index, (source, target) in enumerate(
            (
                (base_hbm, base_ref), (returned_hbm, returned_ref), (after_hbm, after_ref),
                (hidden_hbm, hidden_ref),
            )
        )
    ]
    for copy in loads:
        copy.start()
    place = lax.axis_index("context")
    row = lax.axis_index("expert")
    chip, core = place // 2, lax.rem(place, 2)
    partner = 2 * chip + 1 - core
    barrier = pltpu.get_barrier_semaphore()

    def greet(device):
        pl.semaphore_signal(
            barrier, inc=1, device_id=device, device_id_type=pl.DeviceIdType.MESH
        )

    greet({"context": partner})
    for far in range(1, chips):
        greet({"context": 2 * lax.rem(chip + far, chips) + core})
    for far in range(1, owners):
        greet({"expert": lax.rem(row + far, owners)})
    pl.semaphore_wait(barrier, chips + owners - 1)

    order = list(range(1, chips)) + [0]
    pair = {}
    for item, (source, target) in enumerate(
        ((small_ref, s_twin), (pieces_ref, w_twin), (da_ref, da_twin))
    ):
        for far in order:
            peer = lax.rem(chip + far, chips)
            pair[item, far] = remote(
                source.at[2 * peer + 1 - core], target.at[peer],
                pair_send.at[item, far], pair_recv.at[item, far], {"context": partner},
            )
            pair[item, far].start()

    def across(item, source, target, far):
        peer = lax.rem(chip + far, chips)
        return remote(
            source.at[peer], target.at[chip], chip_send.at[item, far], chip_recv.at[item, far],
            {"context": 2 * peer + core},
        )

    for far in order:
        peer = lax.rem(chip + far, chips)
        mine = 2 * peer + core
        pair[0, far].wait_recv()
        s_sum[peer] = small_ref[mine] + s_twin[peer]
        pair[1, far].wait_recv()
        w_sum[peer] = (
            pieces_ref[mine].astype(F32) + w_twin[peer].astype(F32)
        ).astype(BF16)
    moved = {}
    for far in range(1, chips):
        moved[0, far] = across(0, s_sum, s_in, far)
        moved[0, far].start()
        moved[1, far] = across(1, w_sum, w_in, far)
        moved[1, far].start()
    last = None
    for far in order:
        peer = lax.rem(chip + far, chips)
        pair[2, far].wait_recv()
        da_sum[peer] = (
            da_ref[2 * peer + core].astype(F32) + da_twin[peer].astype(F32)
        ).astype(BF16)
        if last is not None:
            moved[2, last] = across(2, da_sum, da_in, last)
            moved[2, last].start()
        last = far
    for far in range(1, chips):
        moved[0, far].wait_recv()
        moved[1, far].wait_recv()
    s_in[chip] = s_sum[chip]
    w_in[chip] = w_sum[chip]

    width = w_sum.shape[1] // 3
    shard = w_sum.shape[2]
    per_group = chips // groups
    for group in range(groups):
        total = w_in[group * per_group].astype(F32)
        for other in range(1, per_group):
            total = total + w_in[group * per_group + other].astype(F32)
        for which in range(3):
            stack_ref[which * shard : (which + 1) * shard, group * width : (group + 1) * width] = (
                total[which * width : (which + 1) * width].T
            )
    lines = shares.shape[1]
    for owner in range(owners):
        shares[owner] = stack_ref[owner * lines : (owner + 1) * lines, :].astype(BF16)
    total = s_in[0]
    for other in range(1, chips):
        total = total + s_in[other]
    s_total[...] = total
    rows = {}
    for far in range(1, owners):
        peer = lax.rem(row + far, owners)
        rows[0, far] = remote(
            shares.at[peer], shares_in.at[row], row_send.at[0, far], row_recv.at[0, far],
            {"expert": peer},
        )
        rows[0, far].start()
        rows[1, far] = remote(
            s_total, small_all_ref.at[row], row_send.at[1, far], row_recv.at[1, far],
            {"expert": peer},
        )
        rows[1, far].start()
    shares_in[row] = shares[row]
    small_all_ref[row] = total
    for copy in loads:
        copy.wait()
    count = returned_ref.shape[0]
    chunk = 128
    columns_ref[...] = slots_ref[...].T

    def layer(step, carry):
        at = span(step, chunk)
        places = lax.broadcasted_iota(jnp.int32, (chunk, count), 1).astype(F32)
        total = base_ref[at, :]
        for which in range(2):
            hit = (places == columns_ref[at, which : which + 1]).astype(F32).astype(BF16)
            total = total + gates_ref[at, which : which + 1] * dot(hit, returned_ref[...])
        layer_ref[at, :] = total.astype(BF16)
        return carry

    lax.fori_loop(0, layer_ref.shape[0] // chunk, layer, 0)
    for far in range(1, owners):
        rows[0, far].wait_recv()
    summed = shares_in[0].astype(F32)
    for other in range(1, owners):
        summed = summed + shares_in[other].astype(F32)
    block_ref[...] = summed.astype(BF16)
    for far in range(1, chips):
        moved[2, far].wait_recv()
    for far in range(1, owners):
        peer = lax.rem(row + far, owners)
        rows[2, far] = remote(
            block_ref, sums_ref.at[row], row_send.at[2, far], row_recv.at[2, far],
            {"expert": peer},
        )
        rows[2, far].start()
    sums_ref[row] = summed.astype(BF16)
    da_in[chip] = da_sum[chip]

    def input_rows(step, carry):
        at = span(step, chunk)
        total = da_in[0, at, :].astype(F32)
        for other in range(1, chips):
            total = total + da_in[other, at, :].astype(F32)
        grads = total * gain_ref[...]
        values = hidden_ref[at, :].astype(F32)
        inverse = lax.rsqrt(jnp.mean(values * values, axis=1, keepdims=True) + EPS)
        normed = values * inverse
        mean = jnp.mean(grads * normed, axis=1, keepdims=True)
        total_ref[at, :] = after_ref[at, :] + inverse * (grads - normed * mean)
        return carry

    lax.fori_loop(0, layer_ref.shape[0] // chunk, input_rows, 0)
    for far in range(1, owners):
        rows[1, far].wait_recv()
        rows[2, far].wait_recv()
    for owner in range(owners):
        stack_ref[owner * lines : (owner + 1) * lines, :] = sums_ref[owner].astype(F32)
    dots = jnp.zeros((shard, 1), F32)
    for which, (target, weight) in enumerate(
        ((query_ref, query_w), (key_ref, key_w), (value_ref, value_w))
    ):
        grads = stack_ref[which * shard : (which + 1) * shard, :]
        target[...] = grads
        dots = dots + jnp.sum(grads * weight[...].astype(F32), axis=1, keepdims=True)
    dots_ref[...] = dots
    for copy in list(pair.values()) + list(moved.values()) + list(rows.values()):
        copy.wait_send()


def finish(da, pieces, small, small_inputs, bulk, owners, groups, number):
    context, tokens, width = da.shape
    chips = context // 2
    lines, shard = pieces.shape[1:]
    few = small.shape[1]
    stack = 3 * shard
    block = (stack // owners, width)
    return pl.pallas_call(
        functools.partial(finish_kernel, chips, owners, groups),
        out_shape=(
            jax.ShapeDtypeStruct((tokens, width), BF16),
            jax.ShapeDtypeStruct((tokens, width), F32),
            jax.ShapeDtypeStruct((shard, width), F32),
            jax.ShapeDtypeStruct((shard, width), F32),
            jax.ShapeDtypeStruct((shard, width), F32),
            jax.ShapeDtypeStruct((shard, 1), F32),
            jax.ShapeDtypeStruct((owners, few, shard), F32),
        ),
        in_specs=vmem(9) + hbm(4),
        out_specs=vmem(7),
        scratch_shapes=[pltpu.VMEM((owners,) + block, BF16)]
        + [pltpu.VMEM(array.shape, array.dtype) for array in bulk]
        + [
            pltpu.VMEM((tokens, 8), F32),
            pltpu.SemaphoreType.DMA((4,)),
            pltpu.VMEM((chips, tokens, width), BF16),
            pltpu.VMEM((chips, tokens, width), BF16),
            pltpu.VMEM((chips, tokens, width), BF16),
            pltpu.VMEM((chips, lines, shard), BF16),
            pltpu.VMEM((chips, lines, shard), BF16),
            pltpu.VMEM((chips, lines, shard), BF16),
            pltpu.VMEM((chips, few, shard), F32),
            pltpu.VMEM((chips, few, shard), F32),
            pltpu.VMEM((chips, few, shard), F32),
            pltpu.VMEM((few, shard), F32),
            pltpu.VMEM((stack, width), F32),
            pltpu.VMEM((owners,) + block, BF16),
            pltpu.VMEM((owners,) + block, BF16),
            pltpu.VMEM(block, BF16),
            pltpu.SemaphoreType.DMA((3, chips)),
            pltpu.SemaphoreType.DMA((3, chips)),
            pltpu.SemaphoreType.DMA((3, chips)),
            pltpu.SemaphoreType.DMA((3, chips)),
            pltpu.SemaphoreType.DMA((3, owners)),
            pltpu.SemaphoreType.DMA((3, owners)),
        ],
        compiler_params=pltpu.CompilerParams(
            collective_id=number, has_side_effects=True, vmem_limit_bytes=60 << 20
        ),
        name="finish",
    )(da, pieces, small, *small_inputs, *bulk)


def shards(
    hidden_in,
    prior_logits,
    routes,
    block_ids,
    grad_out,
    attn_gain,
    query_weight,
    key_weight,
    value_weight,
    output_weight,
    moe_gain,
    router_weight,
    prior_weight,
    const_mix,
    const_vector,
    gate_weight,
    up_weight,
    down_weight,
):
    token_rows = hidden_in.shape[1]
    model_width = hidden_in.shape[2]
    head_size = model_width // HEADS
    context = lax.axis_size("context")
    owners = lax.axis_size("expert")
    groups = math.gcd(HEADS, context)
    ranks = context // groups
    heads = HEADS // groups
    width = heads * head_size
    length = context * token_rows
    per_owner = gate_weight.shape[0]
    slot_count = per_owner * owners * CAP
    shard_width = model_width // context
    roles = per_owner
    residual = hidden_in[0].astype(F32)
    prior_rows = prior_logits[0]
    route_rows = routes[0]
    cotangent_low = grad_out[0]
    cotangent = cotangent_low.astype(F32)

    half = head_size // 2
    freq = jnp.power(THETA, -2.0 * jnp.arange(half, dtype=F32) / head_size)
    steps = jnp.concatenate(
        [jnp.arange(token_rows), jnp.arange(context) * token_rows]
    ).astype(F32)
    angle = freq[:, None] * steps[None, :]

    gain_row = attn_gain.reshape(1, model_width)
    (
        out_t, log_total, query_t, ids, weights_t, cos_t, sin_t, slots, key_heads, key_t,
        value_heads, a_full, mix_granules, output_full, wide_full, grad_arrived, _,
    ) = attn_forward(
        hidden_in[0], gain_row, block_ids, jnp.transpose(route_rows), cotangent_low,
        jnp.cos(angle), jnp.sin(angle), query_weight, key_weight, value_weight,
        output_weight, gate_weight, up_weight, heads, head_size, ranks, context, owners, roles, 0,
    )
    kept = (out_t, log_total, query_t, key_heads, key_t, value_heads)
    slot_ids = jnp.arange(slot_count).astype(F32)[:, None]
    hit_first = slot_ids == slots[0:1]
    hit_second = slot_ids == slots[1:2]
    pick_either = hit_first.astype(BF16) + hit_second.astype(BF16)
    blocks = (owners, per_owner, CAP, model_width)

    def pick(rows):
        return jnp.dot(pick_either, rows, preferred_element_type=F32).astype(BF16).reshape(blocks)

    out_blocks = mix_granules.reshape(groups, token_rows, width)
    mix_low = jnp.transpose(out_blocks, (1, 0, 2)).reshape(token_rows, model_width)

    after_attn = residual + jnp.dot(mix_low, output_full, preferred_element_type=F32)
    inv_rms2 = lax.rsqrt(jnp.mean(after_attn * after_attn, axis=1, keepdims=True) + EPS)
    normed_two = after_attn * inv_rms2
    moe_input = normed_two * moe_gain
    narrow = jnp.concatenate(
        [router_weight, jnp.transpose(const_mix.reshape(-1, model_width))], axis=1
    )
    narrow_out = jnp.dot(moe_input, narrow, precision=HIGH, preferred_element_type=F32)
    expert_count = router_weight.shape[1]
    consts = const_mix.shape[0]
    logits = narrow_out[:, :expert_count] + jnp.dot(
        prior_rows, prior_weight, precision=HIGH, preferred_element_type=F32
    )
    probs = jax.nn.softmax(logits, axis=1)
    expert_ids = jnp.arange(expert_count, dtype=jnp.int32)
    first_hot = (route_rows[:, 0:1] == expert_ids[None, :]).astype(F32)
    second_hot = (route_rows[:, 1:2] == expert_ids[None, :]).astype(F32)
    chosen = first_hot + second_hot
    gated = probs * chosen
    first_gate = jnp.sum(probs * first_hot, axis=1, keepdims=True)
    second_gate = jnp.sum(probs * second_hot, axis=1, keepdims=True)
    slot_gate = jnp.sum(
        jnp.where(hit_first, first_gate[None, :, 0], 0.0)
        + jnp.where(hit_second, second_gate[None, :, 0], 0.0),
        axis=1,
    )
    def spread(values):
        values = values.reshape(owners, per_owner, CAP)
        return jnp.pad(values, ((0, 0), (0, 8 - per_owner), (0, 128 - CAP)))

    slot_dot, grad_back, expert_out, grad_wide, down_parts = moe(
        spread(slot_gate), pick(moe_input.astype(BF16)), grad_arrived, wide_full, down_weight,
        context, roles, 2,
    )
    slot_dot = slot_dot[:, :, 0, :CAP].reshape(slot_count)
    grad_back = grad_back.reshape(slot_count, model_width)

    const_soft = jax.nn.softmax(narrow_out[:, expert_count:].reshape(token_rows, consts, 2), axis=2)
    const_gate = gated[:, FFN_E + 2 :]
    copy_gate = gated[:, FFN_E + 1 : FFN_E + 2]
    const_out = [
        const_soft[:, c, 0:1] * moe_input + const_soft[:, c, 1:2] * const_vector[c][None, :]
        for c in range(consts)
    ]
    local_moe = copy_gate * moe_input
    for c in range(consts):
        local_moe = local_moe + const_gate[:, c : c + 1] * const_out[c]
    grad_moe_ffn = lax.dot_general(
        pick_either, grad_back, (((0,), (0,)), ((), ())), preferred_element_type=F32
    )
    first_dot = jnp.sum(jnp.where(hit_first, slot_dot[:, None], 0.0), axis=0)[:, None]
    second_dot = jnp.sum(jnp.where(hit_second, slot_dot[:, None], 0.0), axis=0)[:, None]
    copy_dot = jnp.sum(cotangent * moe_input, axis=1, keepdims=True)
    const_dot = [jnp.sum(cotangent * const_out[c], axis=1, keepdims=True) for c in range(consts)]
    extra = jnp.concatenate(
        [jnp.zeros((token_rows, FFN_E + 1), F32), copy_dot, *const_dot], axis=1
    )
    grad_probs = first_hot * first_dot + second_hot * second_dot + chosen * extra
    grad_logits = probs * (grad_probs - jnp.sum(probs * grad_probs, axis=1, keepdims=True))
    grad_prior_rows = lax.dot_general(
        grad_logits, prior_weight, (((1,), (1,)), ((), ())),
        precision=HIGH, preferred_element_type=F32,
    )
    vector_dot = jnp.dot(
        cotangent, jnp.transpose(const_vector), precision=HIGH, preferred_element_type=F32
    )
    grad_soft = jnp.stack(
        [const_gate * copy_dot, const_gate * vector_dot], axis=2
    )
    grad_mix = const_soft * (grad_soft - jnp.sum(const_soft * grad_soft, axis=2, keepdims=True))
    narrow_grad = jnp.concatenate([grad_logits, grad_mix.reshape(token_rows, -1)], axis=1)
    local_scale = copy_gate + jnp.sum(const_soft[:, :, 0] * const_gate, axis=1, keepdims=True)
    grad_moe_input = (
        grad_moe_ffn
        + lax.dot_general(
            narrow_grad, narrow, (((1,), (1,)), ((), ())),
            precision=HIGH, preferred_element_type=F32,
        )
        + local_scale * cotangent
    )
    small_moe = lax.dot_general(
        narrow_grad, moe_input, (((0,), (0,)), ((), ())),
        precision=HIGH, preferred_element_type=F32,
    )
    small_vector = lax.dot_general(
        const_soft[:, :, 1] * const_gate, cotangent, (((0,), (0,)), ((), ())),
        precision=HIGH, preferred_element_type=F32,
    )
    grad_prior_local = lax.dot_general(
        prior_rows, grad_logits, (((0,), (0,)), ((), ())),
        precision=HIGH, preferred_element_type=F32,
    )
    small_gain = jnp.sum(grad_moe_input * normed_two, axis=0, keepdims=True)
    prior_values = jnp.pad(
        grad_prior_local.reshape(-1), (0, -(expert_count * expert_count) % shard_width)
    ).reshape(-1, 1, shard_width)
    prior_lines = prior_values.shape[0]
    small = jnp.concatenate([small_moe, small_vector, small_gain], axis=0)
    small_lines = small.shape[0]
    small = jnp.concatenate(
        [
            small.reshape(small_lines, context, shard_width),
            jnp.broadcast_to(prior_values, (prior_lines, context, shard_width)),
        ],
        axis=0,
    )
    small = jnp.pad(small, ((0, -small.shape[0] % 8), (0, 0), (0, 0)))
    small = jnp.transpose(small, (1, 0, 2))

    grad_normed_two = grad_moe_input * moe_gain
    grad_after = cotangent + inv_rms2 * (
        grad_normed_two - normed_two * jnp.mean(grad_normed_two * normed_two, axis=1, keepdims=True)
    )
    grad_attn_low = grad_after.astype(BF16)
    grad_mix_low = lax.dot_general(
        grad_attn_low, output_full, (((1,), (1,)), ((), ())), preferred_element_type=F32
    ).astype(BF16)
    grad_pieces = jnp.transpose(grad_mix_low.reshape(token_rows, groups, width), (1, 0, 2))
    grad_own = grad_pieces.reshape(-1, TILE // 2, width)
    grad_output_local = lax.dot_general(
        mix_low, grad_attn_low, (((0,), (0,)), ((), ())), preferred_element_type=F32
    ).astype(BF16)
    da_part, w_pieces, output_sum, wide_parts, returned = attn_backward(
        grad_own, a_full, weights_t, cos_t, sin_t, ids, kept,
        grad_wide, expert_out, grad_output_local,
        heads, head_size, ranks, context, roles, 6,
    )
    returned = returned.reshape(slot_count, model_width)
    same = context // 2 // roles
    wide_parts = wide_parts.reshape(roles, same, 2, 2, shard_width, -1)

    def whole(which):
        total = jnp.sum(wide_parts[:, :, :, which].astype(F32), axis=1)
        return jnp.concatenate([total[:, 0], total[:, 1]], axis=-1)

    down_sum = jnp.sum(
        down_parts.reshape(roles, same, -1, model_width).astype(F32), axis=1
    )
    (
        layer_out, grad_input, grad_query, grad_key, grad_value, gain_dots, small_all,
    ) = finish(
        da_part.reshape(context, token_rows, model_width), w_pieces, small,
        (
            slots, jnp.concatenate([first_gate, second_gate], axis=1), gain_row,
            query_weight, key_weight, value_weight,
        ),
        (after_attn + local_moe, returned, grad_after, hidden_in[0]),
        owners, groups, 5,
    )
    small_own = jnp.sum(small_all, axis=0)
    column = lax.axis_index("context") * shard_width
    grad_attn_gain = gain_dots[:, 0] / lax.dynamic_slice_in_dim(attn_gain, column, shard_width)
    mixes = expert_count + 2 * consts
    grad_prior_weight = small_own[small_lines : small_lines + prior_lines].reshape(-1)
    grad_prior_weight = grad_prior_weight[: expert_count * expert_count].reshape(
        expert_count, expert_count
    )
    return (
        layer_out[None],
        grad_input[None],
        grad_prior_rows[None],
        grad_attn_gain,
        grad_query,
        grad_key,
        grad_value,
        output_sum,
        small_own[small_lines - 1],
        jnp.transpose(small_own[:expert_count]),
        grad_prior_weight,
        small_own[expert_count:mixes].reshape(consts, 2, shard_width),
        small_own[mixes : mixes + consts],
        whole(0),
        whole(1),
        down_sum,
    )


def solution(mesh):
    return jax.shard_map(
        shards,
        mesh=mesh,
        in_specs=(
            P("expert", "context", None),
            P("expert", "context", None),
            P("expert", "context", None),
            P("expert", "context"),
            P("expert", "context", None),
            P(),
            P("context", None),
            P("context", None),
            P("context", None),
            P("context", None),
            P(),
            P(),
            P(),
            P(),
            P(),
            P("expert", "context", None),
            P("expert", "context", None),
            P("expert", "context", None),
        ),
        out_specs=(
            P("expert", "context", None),
            P("expert", "context", None),
            P("expert", "context", None),
            P("context"),
            P("context", None),
            P("context", None),
            P("context", None),
            P("context", None),
            P("context"),
            P("context", None),
            P(),
            P(None, None, "context"),
            P(None, "context"),
            P("expert", "context", None),
            P("expert", "context", None),
            P("expert", "context", None),
        ),
        check_vma=False,
    )
```

profile of v0, /device:TPU:0, one launch (start us, length us, event | category | flops | bytes accessed | tf_op | source)
XLA Modules:
  0.0 373.3 jit_solution(17872680064352056706)
XLA Ops:
  0.7 0.5 pad.29.clone
  1.2 1.3 reshape.152.gain_ref
  2.5 0.8 slice_reduce_fusion.10
  3.3 0.8 slice_reduce_fusion.2
  4.1 0.7 reshape.155
  4.8 1.0 multiply_sine_fusion
  5.8 2.1 copy.75
  7.9 90.7 %attn_forward.1 = (f32[192,1536]{1,0:T(8,128)}, f32[3,1536]{1,0:T(4,128)}, bf16[192,1536]{1,0:T(8,128)(2,1)}, f32[8,3072]{1,0:T(8,128)}, bf16[576,768]{1,0:T(8,1...) custom-call(bf16[384,768]{1,0:T(8,128)(2,1)} %bitcast.118, ...), custom_call_target="tpu_custom_call" | custom-call | flops 92000002048 | tf_op jit(solution)/shard_map/attn_forward/pallas_call | solution.py:646
  98.6 1.5 copy.68
  100.1 0.8 slice_reduce_fusion.12
  101.0 2.0 multiply_reduce_fusion.2
  103.1 1.3 fusion.11
  104.6 0.2 fusion.54
  104.9 0.8 fusion.43
  105.8 0.4 fusion.2
  106.2 0.6 fusion.8
  106.9 0.6 pad.12.gates_ref
  107.5 0.8 copy.78.gates_ref
  108.3 2.1 fusion.6
  110.5 1.9 convolution_convert_fusion.1
  112.5 99.3 %moe.1 = (f32[4,2,8,128]{3,2,1,0:T(8,128)}, bf16[4,2,96,768]{3,2,1,0:T(8,128)(2,1)}, bf16[4,2,96,768]{3,2,1,0:T(8,128)(2,1)}, bf16[2,768,1024]{2,1,0:T(8,128)(2,1)}, bf16[4,256,768]{2,1,0:T(8,128)(2,1)}) custom-call(f32[4,8,128]{2,1,0:T(8,128)} %pad.12.gates_ref, bf16[4,2,96,768]{3,2,1,0:T(8,128)(2,1)} %bitcast.129, bf16[16,96,768]{2,1,0:T(8,128)(2,1)} %bitcast.127, ...), custom_call_target="tpu_custom_call" | custom-call | flops 111549997056 | tf_op jit(solution)/shard_map/moe/pallas_call | solution.py:1304
  211.8 0.8 slice_reduce_fusion
  212.6 0.3 fusion.3
  213.0 0.1 multiply_reduce_fusion.3
  213.1 0.2 convolution_bitcast_fusion.1
  213.3 0.1 copy.76
  213.4 0.1 reshape.164
  213.5 0.1 broadcast_in_dim.99
  213.6 0.2 convolution_bitcast_fusion
  213.7 0.6 copy.81
  214.4 0.8 fusion.9
  215.2 0.1 concatenate.39
  215.3 1.2 fusion.31
  216.5 2.1 multiply_reduce_fusion
  218.6 1.7 convert_add_fusion.after_hbm
  220.4 0.7 convolution_convert_fusion.2
  221.1 0.3 copy.73
  221.4 0.7 fusion.30.small_ref
  222.1 1.2 copy.74
  223.3 1.8 convolution_convert_fusion.output_ref
  225.1 77.2 %attn_backward.1 = (bf16[3072,768]{1,0:T(8,128)(2,1)}, bf16[8,576,96]{2,1,0:T(8,128)(2,1)}, f32[96,768]{1,0:T(8,128)}, bf16[8,2,96,1024]{3,2,1,0:T(8,128)(2,1)}, bf16[4,2,96,768]{3,2,1,0:T(8,128)(2,1)}) custom-call(bf16[12,128,192]{2,1,0:T(8,128)(2,1)} %bitcast.116, bf16[3072,768]{1,0:T(8,128)(2,1)} %get-tuple-element.56.a_ref, ...), custom_call_target="tpu_custom_call" | custom-call | flops 69000003584 | tf_op jit(solution)/shard_map/attn_backward/pallas_call | solution.py:895
  302.3 53.5 %finish.1 = (bf16[384,768]{1,0:T(8,128)(2,1)}, f32[384,768]{1,0:T(8,128)}, f32[96,768]{1,0:T(8,128)}, f32[96,768]{1,0:T(8,128)}, f32[96,768]{1,0:T(8,128)}, /*index=5*/f32[96,1]{1,0:T(8,128)}, f32[4,24,96]{2,1,0:T(8,128)}) custom-call(bf16[8,384,768]{2,1,0:T(8,128)(2,1)} %bitcast.108, bf16[8,576,96]{2,1,0:T(8,128)(2,1)} %get-tuple-element.70.pieces_ref, ...), custom_call_target="tpu_custom_call" | custom-call | tf_op jit(solution)/shard_map/finish/pallas_call | solution.py:1551
  355.8 0.9 reduce.17
  356.7 1.3 dynamic-slice_divide_fusion
  358.0 0.8 reduce_sum.196
  358.8 0.5 slice_bitcast_fusion.7
  359.3 0.6 slice.148
  359.9 0.6 fusion.53
  360.4 0.6 slice_bitcast_fusion.4
  361.0 0.7 slice.120
  361.7 1.4 convert_reduce_fusion
  363.1 1.0 copy-done.3
  364.2 0.8 convert_reduce_fusion.1
  364.9 0.4 slice_bitcast_fusion.1
  365.3 1.2 pad_maximum_fusion.1
  366.6 1.2 pad_maximum_fusion
  367.8 0.8 copy.112
  368.7 0.7 copy-done.8
  369.3 1.0 copy.113
  370.3 0.1 copy-done.15
  370.5 0.7 copy.114
  371.2 0.7 copy.115
  371.9 0.7 copy.116
  372.6 0.7 copy.117
  (82 shorter events, 0.9 us)
Async XLA Ops:
  0.6 103.9 %copy-start = (f32[12,12]{1,0:T(8,128)S(1)}, f32[12,12]{1,0:T(8,128)}, u32[]{:S(2)}) copy-start(f32[12,12]{1,0:T(8,128)} %param.30) | copy-start | bytes 1732
  98.6 2.4 copy-start.10
  100.1 0.8 copy-start.5
  100.9 2.1 copy-start.16
  101.0 2.1 copy-start.18
  103.0 1.6 copy-start.17
  103.0 1.9 copy-start.4
  103.0 3.2 copy-start.2
  103.0 3.2 copy-start.19
  112.5 100.5 %copy-start.20 = (f32[12]{0:T(128)S(1)}, f32[12]{0:T(128)}, u32[]{:S(2)}) copy-start(f32[12]{0:T(128)} %pad.29.clone) | copy-start | bytes 148
  214.4 2.1 copy-start.21
  218.6 1.8 copy-start.9
  220.4 2.9 copy-start.1
  221.1 2.2 copy-start.6
  302.3 59.4 %copy-start.7 = (bf16[4,256,768]{2,1,0:T(8,128)(2,1)S(1)}, bf16[4,256,768]{2,1,0:T(8,128)(2,1)}, u32[]{:S(2)}) copy-start(bf16[4,256,768]{2,1,0:T(8,128)(2,1)} %get-tuple-element.81) | copy-start | bytes 4718596
  361.7 2.5 copy-start.3
  366.6 1.3 copy-start.11
  367.8 1.5 copy-start.8
  369.3 1.1 copy-start.15
  369.3 1.8 copy-start.14
  369.3 2.6 copy-start.13
  370.4 2.2 copy-start.12
where the time goes:
time: 374 us; the launch traced here: 373 us
  Pallas kernels  321 us (86%)
  local copies, waits for them, and re-layouts  23.5 us (6%)
  other arithmetic  14.3 us (4%)
  matrix products  13.7 us (4%)
    pallas_call x1, Pallas kernels, moe(): pl.pallas_call(functools.partial(moe_kernel, context, owners, roles, squa...  99.3 us
    pallas_call x1, Pallas kernels, attn_forward(): pl.pallas_call(functools.partial(attn_forward_kernel, dims), out_shape=sh...  90.7 us
    pallas_call x1, Pallas kernels, attn_backward(): pl.pallas_call(functools.partial(attn_backward_kernel, dims), out_shape=s...  77.2 us
    pallas_call x1, Pallas kernels, finish(): pl.pallas_call(functools.partial(finish_kernel, chips, owners, groups), o...  53.5 us

commit v1 on v0

--- a/solution.py
+++ b/solution.py
@@ -690,10 +690,12 @@
 
 def attn_backward_kernel(
     dims,
-    grad_ref, a_ref, wt_ref, cos_ref, sin_ref, ids_all_ref,
-    out_t_ref, lse_ref, query_t_ref, key_ref, key_t_ref, value_ref,
+    grad_ref, a_hbm, wt_hbm, cos_hbm, sin_hbm, ids_hbm,
+    out_t_hbm, lse_hbm, query_t_hbm, key_hbm, key_t_hbm, value_hbm,
     wide_ref, outs_ref, output_ref,
-    da_ref, pieces_ref, output_sum_ref, wide_in_ref, outs_in_ref,
+    da_out, pieces_ref, output_sum_ref, wide_in_ref, outs_in_ref,
+    a_ref, wt_ref, cos_ref, sin_ref, ids_all_ref,
+    out_t_ref, lse_ref, query_t_ref, key_ref, key_t_ref, value_ref, da_ref, load_sem, da_sem,
     query_ref, own_grad_ref, dq_ref, dk_ref, dv_ref, grad_w_ref,
     landed_ref, output_in_ref, share_ref, shares_ref,
     granule_send, granule_recv, share_send, share_recv,
@@ -707,6 +709,19 @@
     tiles = length // TILE
     own_tiles = tiles // ranks
     chips = context // 2
+    loads = [
+        pltpu.make_async_copy(source, target, load_sem.at[index])
+        for index, (source, target) in enumerate(
+            (
+                (key_hbm, key_ref), (value_hbm, value_ref), (key_t_hbm, key_t_ref),
+                (query_t_hbm, query_t_ref), (out_t_hbm, out_t_ref), (lse_hbm, lse_ref),
+                (ids_hbm, ids_all_ref), (cos_hbm, cos_ref), (sin_hbm, sin_ref),
+                (a_hbm, a_ref), (wt_hbm, wt_ref),
+            )
+        )
+    ]
+    for copy in loads:
+        copy.start()
     place, row = meet(context, owners)
     chip, core = place // 2, lax.rem(place, 2)
     owned = landed_ref.shape[0]
@@ -775,6 +790,8 @@
     lax.fori_loop(0, owned, landed, 0)
     for copy in output_copies + copies:
         copy.start()
+    for copy in loads:
+        copy.wait()
 
     def share_copy(far):
         return remote(
@@ -854,13 +871,28 @@
         grad_w_ref[width:, :] += dot(both.astype(BF16), a_ref[at, :])
         total = da_ref[at, :].astype(F32) + dot(both.T.astype(BF16), wt_ref[width:, :])
         da_ref[at, :] = total.astype(BF16)
+
+        @pl.when(step > 0)
+        def _():
+            keep(step - 1).start()
+
+        return carry
+
+    def keep(step):
+        at = lanes(step)
+        return pltpu.make_async_copy(da_ref.at[at, :], da_out.at[at, :], da_sem.at[step])
+
+    def kept(step, carry):
+        keep(step).wait()
         return carry
 
     lax.fori_loop(0, tiles, finish, 0)
     for piece in range(pieces_ref.shape[0]):
         pieces_ref[piece] = grad_w_ref[:, piece * shard : (piece + 1) * shard].astype(BF16)
+    keep(tiles - 1).start()
     for copy in copies:
         copy.wait()
+    lax.fori_loop(0, tiles, kept, 0)
     for far in range(1, owners):
         share_copy(far).wait()
     shares_ref[row] = share_ref[...]
@@ -895,9 +927,15 @@
     return pl.pallas_call(
         functools.partial(attn_backward_kernel, dims),
         out_shape=shapes,
-        in_specs=vmem(12) + hbm(3),
-        out_specs=vmem(3) + hbm(2),
+        in_specs=hbm(15),
+        out_specs=hbm(1) + vmem(2) + hbm(2),
         scratch_shapes=[
+            pltpu.VMEM(array.shape, array.dtype)
+            for array in (a_full, weights_t, cos_t, sin_t, ids) + kept + (a_full,)
+        ]
+        + [
+            pltpu.SemaphoreType.DMA((11,)),
+            pltpu.SemaphoreType.DMA((length // TILE,)),
             pltpu.VMEM((heads, TILE, size), BF16),
             pltpu.VMEM((heads, TILE, size), BF16),
             pltpu.VMEM((width, TILE), F32),
@@ -1356,11 +1394,19 @@
     da_ref, pieces_ref, small_ref, slots_ref, gates_ref, gain_ref, query_w, key_w, value_w,
     base_hbm, returned_hbm, after_hbm, hidden_hbm,
     layer_ref, total_ref, query_ref, key_ref, value_ref, dots_ref, small_all_ref,
-    sums_ref, base_ref, returned_ref, after_ref, hidden_ref, columns_ref, load_sem,
+    sums_ref, base_ref, returned_ref, after_ref, hidden_ref, columns_ref, da_own, load_sem,
+    own_sem,
     da_twin, da_sum, da_in, w_twin, w_sum, w_in, s_twin, s_sum, s_in, s_total,
     stack_ref, shares, shares_in, block_ref,
     pair_send, pair_recv, chip_send, chip_recv, row_send, row_recv,
 ):
+    own_core = lax.rem(lax.axis_index("context"), 2)
+    owns = [
+        pltpu.make_async_copy(da_ref.at[2 * index + own_core], da_own.at[index], own_sem.at[index])
+        for index in range(chips)
+    ]
+    for copy in owns:
+        copy.start()
     loads = [
         pltpu.make_async_copy(source, target, load_sem.at[index])
         for index, (source, target) in enumerate(
@@ -1426,11 +1472,13 @@
         moved[1, far] = across(1, w_sum, w_in, far)
         moved[1, far].start()
     last = None
+    for copy in owns:
+        copy.wait()
     for far in order:
         peer = lax.rem(chip + far, chips)
         pair[2, far].wait_recv()
         da_sum[peer] = (
-            da_ref[2 * peer + core].astype(F32) + da_twin[peer].astype(F32)
+            da_own[peer].astype(F32) + da_twin[peer].astype(F32)
         ).astype(BF16)
         if last is not None:
             moved[2, last] = across(2, da_sum, da_in, last)
@@ -1559,13 +1607,15 @@
             jax.ShapeDtypeStruct((shard, 1), F32),
             jax.ShapeDtypeStruct((owners, few, shard), F32),
         ),
-        in_specs=vmem(9) + hbm(4),
+        in_specs=hbm(1) + vmem(8) + hbm(4),
         out_specs=vmem(7),
         scratch_shapes=[pltpu.VMEM((owners,) + block, BF16)]
         + [pltpu.VMEM(array.shape, array.dtype) for array in bulk]
         + [
             pltpu.VMEM((tokens, 8), F32),
+            pltpu.VMEM((chips, tokens, width), BF16),
             pltpu.SemaphoreType.DMA((4,)),
+            pltpu.SemaphoreType.DMA((chips,)),
             pltpu.VMEM((chips, tokens, width), BF16),
             pltpu.VMEM((chips, tokens, width), BF16),
             pltpu.VMEM((chips, tokens, width), BF16),

time: 374 us -> 367 us (0.981)
  Pallas kernels: 321 us -> 314 us
    pallas_call x1, Pallas kernels: 77.2 us -> 71.5 us  [attn_backward(): pl.pallas_call(functools.partial(attn_backward_kernel, dims), out_shape=s...]
where the time goes in v1:
time: 367 us; the launch traced here: 366 us
  Pallas kernels  314 us (86%)
  local copies, waits for them, and re-layouts  23.5 us (6%)
  other arithmetic  14.3 us (4%)
  matrix products  13.7 us (4%)
    pallas_call x1, Pallas kernels, moe(): pl.pallas_call(functools.partial(moe_kernel, context, owners, roles, squa...  99.3 us
    pallas_call x1, Pallas kernels, attn_forward(): pl.pallas_call(functools.partial(attn_forward_kernel, dims), out_shape=sh...  90.7 us
    pallas_call x1, Pallas kernels, attn_backward(): pl.pallas_call(functools.partial(attn_backward_kernel, dims), out_shape=s...  71.5 us
    pallas_call x1, Pallas kernels, finish(): pl.pallas_call(functools.partial(finish_kernel, chips, owners, groups), o...  52.3 us

profile of v1, /device:TPU:0, one launch (start us, length us, event | category | flops | bytes accessed | tf_op | source)
XLA Modules:
  0.0 366.4 jit_solution(4420064487841933155)
XLA Ops:
  0.7 0.5 pad.29.clone
  1.2 1.3 reshape.152.gain_ref
  2.5 0.8 slice_reduce_fusion.10
  3.3 0.8 slice_reduce_fusion.2
  4.1 0.7 reshape.155
  4.8 1.0 multiply_sine_fusion
  5.8 2.1 copy.75
  7.9 90.7 %attn_forward.1 = (f32[192,1536]{1,0:T(8,128)}, f32[3,1536]{1,0:T(4,128)}, bf16[192,1536]{1,0:T(8,128)(2,1)}, f32[8,3072]{1,0:T(8,128)}, bf16[576,768]{1,0:T(8,1...) custom-call(bf16[384,768]{1,0:T(8,128)(2,1)} %bitcast.118, ...), custom_call_target="tpu_custom_call" | custom-call | flops 92000002048 | tf_op jit(solution)/shard_map/attn_forward/pallas_call | solution.py:646
  98.6 1.5 copy.68
  100.1 0.8 slice_reduce_fusion.12
  101.0 2.0 multiply_reduce_fusion.2
  103.1 1.3 fusion.11
  104.6 0.2 fusion.54
  104.9 0.8 fusion.43
  105.8 0.4 fusion.2
  106.2 0.6 fusion.8
  106.9 0.6 pad.12.gates_ref
  107.5 0.8 copy.78.gates_ref
  108.3 2.1 fusion.6
  110.5 1.9 convolution_convert_fusion.1
  112.5 99.3 %moe.1 = (f32[4,2,8,128]{3,2,1,0:T(8,128)}, bf16[4,2,96,768]{3,2,1,0:T(8,128)(2,1)}, bf16[4,2,96,768]{3,2,1,0:T(8,128)(2,1)}, bf16[2,768,1024]{2,1,0:T(8,128)(2,1)}, bf16[4,256,768]{2,1,0:T(8,128)(2,1)}) custom-call(f32[4,8,128]{2,1,0:T(8,128)} %pad.12.gates_ref, bf16[4,2,96,768]{3,2,1,0:T(8,128)(2,1)} %bitcast.129, bf16[16,96,768]{2,1,0:T(8,128)(2,1)} %bitcast.127, ...), custom_call_target="tpu_custom_call" | custom-call | flops 111549997056 | tf_op jit(solution)/shard_map/moe/pallas_call | solution.py:1342
  211.8 0.8 slice_reduce_fusion
  212.6 0.3 fusion.3
  213.0 0.1 multiply_reduce_fusion.3
  213.1 0.2 convolution_bitcast_fusion.1
  213.3 0.1 copy.76
  213.4 0.1 reshape.164
  213.5 0.1 broadcast_in_dim.99
  213.6 0.2 convolution_bitcast_fusion
  213.7 0.6 copy.81
  214.4 0.8 fusion.9
  215.2 0.1 concatenate.39
  215.3 1.2 fusion.31
  216.5 2.1 multiply_reduce_fusion
  218.6 1.7 convert_add_fusion.after_hbm
  220.4 0.7 convolution_convert_fusion.2
  221.1 0.3 copy.73
  221.4 0.7 fusion.30.small_ref
  222.1 1.2 copy.74
  223.3 1.8 convolution_convert_fusion.output_ref
  225.1 71.5 %attn_backward.1 = (bf16[3072,768]{1,0:T(8,128)(2,1)}, bf16[8,576,96]{2,1,0:T(8,128)(2,1)}, f32[96,768]{1,0:T(8,128)}, bf16[8,2,96,1024]{3,2,1,0:T(8,128)(2,1)}, bf16[4,2,96,768]{3,2,1,0:T(8,128)(2,1)}) custom-call(bf16[12,128,192]{2,1,0:T(8,128)(2,1)} %bitcast.116, bf16[3072,768]{1,0:T(8,128)(2,1)} %get-tuple-element.56.a_hbm, ...), custom_call_target="tpu_custom_call" | custom-call | flops 69000003584 | tf_op jit(solution)/shard_map/attn_backward/pallas_call | solution.py:927
  296.6 52.3 %finish.1 = (bf16[384,768]{1,0:T(8,128)(2,1)}, f32[384,768]{1,0:T(8,128)}, f32[96,768]{1,0:T(8,128)}, f32[96,768]{1,0:T(8,128)}, f32[96,768]{1,0:T(8,128)}, /*index=5*/f32[96,1]{1,0:T(8,128)}, f32[4,24,96]{2,1,0:T(8,128)}) custom-call(bf16[8,384,768]{2,1,0:T(8,128)(2,1)} %bitcast.108, bf16[8,576,96]{2,1,0:T(8,128)(2,1)} %get-tuple-element.70.pieces_ref, ...), custom_call_target="tpu_custom_call" | custom-call | tf_op jit(solution)/shard_map/finish/pallas_call | solution.py:1599
  348.9 0.9 reduce.17
  349.8 1.3 dynamic-slice_divide_fusion
  351.1 0.8 reduce_sum.196
  351.9 0.5 slice_bitcast_fusion.7
  352.4 0.6 slice.148
  353.0 0.6 fusion.53
  353.6 0.6 slice_bitcast_fusion.4
  354.2 0.7 slice.120
  354.8 1.4 convert_reduce_fusion
  356.3 1.0 copy-done.3
  357.3 0.8 convert_reduce_fusion.1
  358.1 0.4 slice_bitcast_fusion.1
  358.5 1.2 pad_maximum_fusion.1
  359.7 1.2 pad_maximum_fusion
  361.0 0.8 copy.112
  361.8 0.7 copy-done.8
  362.5 1.0 copy.113
  363.5 0.1 copy-done.15
  363.6 0.7 copy.114
  364.3 0.7 copy.115
  365.0 0.7 copy.116
  365.7 0.7 copy.117
  (82 shorter events, 0.9 us)
Async XLA Ops:
  0.6 103.9 %copy-start = (f32[12,12]{1,0:T(8,128)S(1)}, f32[12,12]{1,0:T(8,128)}, u32[]{:S(2)}) copy-start(f32[12,12]{1,0:T(8,128)} %param.30) | copy-start | bytes 1732
  98.6 2.4 copy-start.10
  100.1 0.8 copy-start.5
  100.9 2.1 copy-start.16
  101.0 2.1 copy-start.18
  103.0 1.6 copy-start.17
  103.0 1.9 copy-start.4
  103.0 3.2 copy-start.2
  103.0 3.2 copy-start.19
  112.5 100.5 %copy-start.20 = (f32[12]{0:T(128)S(1)}, f32[12]{0:T(128)}, u32[]{:S(2)}) copy-start(f32[12]{0:T(128)} %pad.29.clone) | copy-start | bytes 148
  214.4 2.1 copy-start.21
  218.6 1.8 copy-start.9
  220.4 2.9 copy-start.1
  221.1 2.2 copy-start.6
  296.6 58.3 %copy-start.7 = (bf16[4,256,768]{2,1,0:T(8,128)(2,1)S(1)}, bf16[4,256,768]{2,1,0:T(8,128)(2,1)}, u32[]{:S(2)}) copy-start(bf16[4,256,768]{2,1,0:T(8,128)(2,1)} %get-tuple-element.81) | copy-start | bytes 4718596
  354.8 2.5 copy-start.3
  359.7 1.3 copy-start.11
  361.0 1.5 copy-start.8
  362.4 1.1 copy-start.15
  362.4 1.8 copy-start.14
  362.4 2.6 copy-start.13
  363.6 2.2 copy-start.12
